TPU v7x, 32 devices: a whole 2x2x4 slice. The times are simulated.
32 devices in a mesh: group: 4 (over x, core), theta: 4 (over z), radial: 2 (over y).
Axes of the slice: x: 2, y: 2, z: 4, core: 2. Of those that a mesh axis runs over, the one named last changes fastest.
Arguments:
- scalars: float32 [26, 16, 16, 2048], P(None, 'group', 'radial', 'theta'), may hold values from 0.1 to 2
- axial_speed: float32 [16, 16, 2048], P('group', 'radial', 'theta'), may hold values from 0.2 to 0.9
- mixing: float32 [16, 16, 2048], P('group', 'radial', 'theta'), may hold values from 0.02 to 0.12
- reaction_rate: float32 [16, 16, 2048], P('group', 'radial', 'theta'), may hold values from 0.05 to 0.5
- reaction: float32 [20, 20], replicated, may hold values from -1.25 to 1.25
- nucleation: float32 [6], replicated, may hold values from 0.1 to 1
- coagulation: float32 [6], replicated, may hold values from 0.05 to 0.5
- inflow: float32 [26, 16, 2048], P(None, 'radial', 'theta'), may hold values from 0.1 to 2
- tile_weights: float32 [16, 128, 128], P('theta'), may hold values from -0.5 to 0.5
- donor_shift: int32 [16], P('theta'), may hold values from -1 to 1, as said below
- rotor_offset: int32 [1], replicated, may hold values from 0 to 2047
Outputs:
- advanced: float32 [26, 16, 16, 2048], P(None, 'group', 'radial', 'theta')
Inputs may be any that keep to these rules, and one draw needn't show every extreme that they name: `donor_shift`: in every aligned block of 4 tiles the first tile has offset -1 and the last offset 1.
All inputs are finite; a program needn't handle non-finite values.
Results may differ from a plain program's by a relative error of at most 0.00005.
Values sent between devices are 32-bit elements; how exact they have to be, the bound alone decides.
No kernel may reach another device: no remote copies, remote signals or barrier semaphores. Data moves between devices by JAX's collectives and lax.ppermute only.
A program may use at most 64 MiB of HBM per device.

v0:
```python
import jax
import jax.numpy as jnp
from jax import lax
from jax.sharding import PartitionSpec as P

SPECIES = 20


highest = lax.Precision.HIGHEST


def from_behind(block, axis, distance):
    devices = range(lax.axis_size(axis))
    route = [((i - distance) % len(devices), i) for i in devices]
    return lax.ppermute(block, axis, route)


def padded(array, sides, width, wrap):
    for axis, dim in sides:
        count, length = (lax.axis_size(axis), array.shape[dim])
        up = [(i, (i + 1) % count) for i in range(count if wrap else count - 1)]
        down = [(j, i) for i, j in up]
        last = lax.slice_in_dim(array, length - width, length, axis=dim)
        initial = lax.slice_in_dim(array, 0, width, axis=dim)
        before = lax.ppermute(last, axis, up)
        after = lax.ppermute(initial, axis, down)
        array = jnp.concatenate([before, array, after], axis=dim)
    return array


def from_behind_2(array, axis, by):
    count = lax.axis_size(axis)
    pairs = [(i, i + by) for i in range(count) if 0 <= i + by < count]
    return lax.ppermute(array, axis, pairs)


def rotate_rows(plane_rows, rotor_offset):
    sectors = lax.axis_size("theta")
    theta_cells = plane_rows.shape[1]
    device_hops = rotor_offset[0] // theta_cells
    cell_shift = rotor_offset[0] % theta_cells
    scattered = lax.all_to_all(plane_rows[None], "theta", split_axis=2, concat_axis=0, tiled=True)
    doubled = jnp.concatenate([scattered, scattered], axis=0)
    turned = lax.dynamic_slice_in_dim(doubled, sectors - device_hops, sectors, 0)
    shifted = lax.all_to_all(turned, "theta", split_axis=0, concat_axis=2, tiled=True)[0]
    previous = from_behind(shifted, "theta", 1)
    joined = jnp.concatenate([previous, shifted], axis=1)
    return lax.dynamic_slice_in_dim(joined, theta_cells - cell_shift, theta_cells, 1)


def apply_tiles(picked_rows, tile_weights):
    row_count, theta_cells = picked_rows.shape
    tile_blocks = picked_rows.reshape(row_count, theta_cells // 128, 128)
    result = jnp.einsum("rtk,tjk->rtj", tile_blocks, tile_weights, precision=highest)
    return result.reshape(row_count, theta_cells)


def couple_cells(plane_rows, tile_weights, donor_shift, rotor_offset):
    row_count, theta_cells = plane_rows.shape
    tile_count = theta_cells // 128
    rotated = rotate_rows(plane_rows, rotor_offset)
    extended = padded(rotated, (("theta", 1),), 128, True)
    tile_blocks = extended.reshape(row_count, tile_count + 2, 128)
    columns = lax.broadcasted_iota(jnp.int32, (tile_count, tile_count + 2), 1)
    targets = (
        lax.broadcasted_iota(jnp.int32, (tile_count, tile_count + 2), 0) + 1 + donor_shift[:, None]
    )
    chooser = (columns == targets).astype(jnp.float32)
    picked = jnp.einsum("rsk,ts->rtk", tile_blocks, chooser, precision=highest)
    return apply_tiles(picked.reshape(row_count, theta_cells), tile_weights)


def couple_rows(plane_rows, tile_weights, donor_shift, rotor_offset):
    return couple_cells(plane_rows, tile_weights, donor_shift, rotor_offset)


def local(
    scalars,
    axial_speed,
    mixing,
    reaction_rate,
    reaction,
    nucleation,
    coagulation,
    inflow,
    tile_weights,
    donor_shift,
    rotor_offset,
):
    variables, layers, radial_cells, theta_cells = scalars.shape
    groups = lax.axis_size("group")
    group_index = lax.axis_index("group")
    row_count = variables * radial_cells
    last_layer = scalars[:, layers - 1]
    received = from_behind_2(last_layer, "group", 1)
    coupled = couple_rows(
        received.reshape(row_count, theta_cells), tile_weights, donor_shift, rotor_offset
    )
    coupled = coupled.reshape(variables, radial_cells, theta_cells)
    ghost_plane = jnp.where(
        group_index == 0, inflow, jnp.where(group_index == groups - 1, coupled, received)
    )
    upstream = jnp.concatenate([ghost_plane[:, None], scalars[:, :-1]], axis=1)
    circle = padded(scalars, (("theta", 3),), 1, True)
    walls = padded(scalars, (("radial", 2),), 1, False)
    beside_all = circle[:, :, :, :-2] + circle[:, :, :, 2:]
    beside_all = beside_all + walls[:, :, 2:] + walls[:, :, :-2]
    laplace_term = beside_all - 4.0 * scalars
    species = scalars[:SPECIES]
    moments = scalars[SPECIES:]
    produced = jnp.dot(
        reaction,
        species.reshape(SPECIES, -1),
        precision=highest,
        preferred_element_type=jnp.float32,
    ).reshape(species.shape)
    growth = (
        nucleation[:, None, None, None] * species[SPECIES - 1]
        - coagulation[:, None, None, None] * moments[0] * moments
    )
    sources = jnp.concatenate([produced, growth], axis=0) * reaction_rate
    return scalars - axial_speed * (scalars - upstream) + mixing * laplace_term + sources


def solution(mesh):
    placed = (
        P(None, "group", "radial", "theta"),
        P("group", "radial", "theta"),
        P("group", "radial", "theta"),
        P("group", "radial", "theta"),
        P(),
        P(),
        P(),
        P(None, "radial", "theta"),
        P("theta", None, None),
        P("theta"),
        P(),
    )
    return jax.shard_map(
        local,
        mesh=mesh,
        in_specs=placed,
        out_specs=P(None, "group", "radial", "theta"),
        check_vma=False,
    )
```

profile of v0, /device:TPU:2, one launch (start us, length us, event | category | flops | bytes accessed | tf_op | source)
XLA Modules:
  0.0 98.0 jit_solution(16897832875728588099)
XLA Ops:
  0.0 0.0 copy-start
  0.0 2.5 %copy.82 = f32[26,4,8,512]{3,0,2,1:T(8,128)S(1)} copy(f32[26,4,8,512]{3,2,1,0:T(8,128)} %param.11) | data formatting | bytes 3407872 | tf_op args[0]
  2.5 0.0 copy-start.1
  2.6 1.9 %collective-permute-start = (f32[26,8,512]{2,0,1:T(8,128)S(1)}, f32[26,8,512]{2,0,1:T(8,128)S(1)}, u32[]{:S(2)}, u32[]{:S(2)}) collective-permute-start(f32[26,8,512]{2,0,1:T(8,128)S(1)} %slice_bitcast_fusion.2), channel_id=1, source_target_pairs={{0,8},{8,16},{16,24},{1,9},{9,17},{17,25},{2,10},{10,18},{18,26},{... | collective-permute-start | bytes 1277960 | tf_op jit(solution)/shard_map/ppermute | solution.py:34
  4.5 8.6 %collective-permute-done = f32[26,8,512]{2,0,1:T(8,128)S(1)} collective-permute-done((f32[26,8,512]{2,0,1:T(8,128)S(1)}, f32[26,8,512]{2,0,1:T(8,128)S(1)}, u32[]{:S(2)}, u32[]{:S(2)}) %collective-permute-start) | collective-permute-done | bytes 426016 | tf_op jit(solution)/shard_map/ppermute | solution.py:34
  13.1 0.8 copy-done.4
  13.8 0.3 copy.112
  14.1 1.0 %copy.73 = f32[1,208,512]{1,0,2:T(1,128)} copy(f32[1,208,512]{2,1,0:T(8,128)S(1)} %bitcast.63) | data formatting | bytes 851968 | tf_op jit(solution)/shard_map/broadcast_in_dim;reshape | solution.py:42
  15.1 4.9 %all-to-all-start = ((f32[1,208,512]{1,0,2:T(1,128)}), f32[1,208,512]{1,0,2:T(1,128)S(1)}, u32[]{:S(2)}, u32[]{:S(2)}) async-start(f32[1,208,512]{1,0,2:T(1,128)} %copy.73), calls=%async_computation | async-start | bytes 1048576 | tf_op jit(solution)/shard_map/all_to_all | solution.py:42
  20.0 0.8 fusion.21
  20.8 1.3 %collective-permute-start.6 = (f32[26,4,1,512]{3,0,2,1:T(8,128)}, f32[26,4,1,512]{3,0,2,1:T(8,128)}, u32[]{:S(2)}, u32[]{:S(2)}) collective-permute-start(f32[26,4,1,512]{3,0,2,1:T(8,128)} %get-tuple-element.7), channel_id=1, source_target_pairs={{1,0},{3,2},{5,4},{7,6},{9,8},{11,10},{13,12},{15,14},{17,16},{19,... | collective-permute-start | bytes 638984 | tf_op jit(solution)/shard_map/ppermute | solution.py:26
  22.1 0.0 copy-start.9
  22.1 0.0 copy-start.10
  22.2 6.1 %collective-permute-start.7 = (f32[26,4,1,512]{3,0,2,1:T(8,128)}, f32[26,4,1,512]{3,0,2,1:T(8,128)}, u32[]{:S(2)}, u32[]{:S(2)}) collective-permute-start(f32[26,4,1,512]{3,0,2,1:T(8,128)} %get-tuple-element.8), channel_id=1, source_target_pairs={{0,1},{2,3},{4,5},{6,7},{8,9},{10,11},{12,13},{14,15},{16,17},{18,... | collective-permute-start | bytes 638984 | tf_op jit(solution)/shard_map/ppermute | solution.py:25
  28.2 1.1 %fusion.20 = (f32[26,4,8,1]{3,0,2,1:T(8,128)}, f32[26,4,8,1]{3,0,2,1:T(8,128)}) fusion(f32[26,4,8,512]{3,0,2,1:T(8,128)S(1)} %copy.82), kind=kLoop, calls=%fused_computation.44 | loop fusion | bytes 13312 | tf_op jit(solution)/shard_map/slice | solution.py:23
  29.4 2.0 %collective-permute-start.4 = (f32[26,4,8,1]{3,0,2,1:T(8,128)}, f32[26,4,8,1]{3,0,2,1:T(8,128)}, u32[]{:S(2)}, u32[]{:S(2)}) collective-permute-start(f32[26,4,8,1]{3,0,2,1:T(8,128)} %get-tuple-element.5), channel_id=1, source_target_pairs={{0,2},{2,4},{4,6},{6,0},{1,3},{3,5},{5,7},{7,1},{8,10},{10,12},{12... | collective-permute-start | bytes 9992 | tf_op jit(solution)/shard_map/ppermute | solution.py:25
  32.1 8.1 %all-to-all-done = f32[1,208,512]{1,0,2:T(1,128)S(1)} async-done(((f32[1,208,512]{1,0,2:T(1,128)}), f32[1,208,512]{1,0,2:T(1,128)S(1)}, u32[]{:S(2)}, u32[]{:S(2)}) %all-to-all-start) | async-done | bytes 426016 | tf_op jit(solution)/shard_map/all_to_all | solution.py:42
  40.1 0.3 copy.74
  40.5 0.8 fusion.14
  41.3 3.5 %all-to-all-start.1 = ((f32[4,208,128]{2,1,0:T(8,128)}), f32[4,208,128]{2,1,0:T(8,128)S(1)}, u32[]{:S(2)}, u32[]{:S(2)}) async-start(f32[4,208,128]{2,1,0:T(8,128)} %fusion.14), calls=%async_computation.1 | async-start | bytes 851968 | tf_op jit(solution)/shard_map/all_to_all | solution.py:45
  44.8 0.9 slice_bitcast_fusion.4
  45.7 0.0 copy-done.9
  45.7 0.0 copy-done.10
  45.7 1.0 %fusion.11 = f32[6,4,8,512]{3,0,2,1:T(8,128)} fusion(f32[26,4,8,512]{3,0,2,1:T(8,128)S(1)} %copy.82, f32[4,8,512]{2,1,0:T(8,128)S(1)} %get-tuple-element.10, f32[6]{0:T(128)S(1)} %copy-done.9, f32[4,8,512]{2,1,0:T(8,128)S(1)} %get-tuple-element.9, f32[6]{0:T(128)S(1)} %copy-done.10), kind=kLoop, calls=%fused_computation.27 | loop fusion | flops 393216 | bytes 917552 | tf_op jit(solution)/shard_map/sub | solution.py:118
  46.7 2.5 %slice_bitcast_fusion.1 = f32[20,32,512]{2,1,0:T(8,128)} fusion(f32[26,4,8,512]{3,2,1,0:T(8,128)} %param.11), kind=kLoop, calls=%fused_computation.18 | loop fusion | bytes 2621440
  49.2 9.3 %all-to-all-done.1 = f32[4,208,128]{2,1,0:T(8,128)S(1)} async-done(((f32[4,208,128]{2,1,0:T(8,128)}), f32[4,208,128]{2,1,0:T(8,128)S(1)}, u32[]{:S(2)}, u32[]{:S(2)}) %all-to-all-start.1) | async-done | bytes 426016 | tf_op jit(solution)/shard_map/all_to_all | solution.py:45
  58.5 0.2 copy.75
  58.7 0.1 collective-permute-start.1
  58.8 1.0 %copy-done.3 = f32[20,32,512]{2,1,0:T(8,128)S(1)} copy-done((f32[20,32,512]{2,1,0:T(8,128)S(1)}, f32[20,32,512]{2,1,0:T(8,128)}, u32[]{:S(2)}) %copy-start.3) | copy-done | bytes 1310744
  59.8 0.1 slice_bitcast_fusion
  60.0 0.0 copy-done.8
  60.0 0.0 copy-start.11
  60.0 3.2 %fusion.9 = f32[20,4,8,512]{3,0,2,1:T(8,128)} fusion(f32[4,8,512,20]{2,1,0,3:T(8,128)S(1)} %slice_bitcast_fusion, f32[20,20]{1,0:T(8,128)S(1)} %copy-done.8), kind=kOutput, calls=%fused_computation.15 | convolution fusion | flops 78643200 | bytes 2623040 | tf_op jit(solution)/shard_map/dot_general | solution.py:111
  63.2 10.1 %collective-permute-done.1 = f32[208,512]{1,0:T(8,128)S(1)} collective-permute-done((f32[208,512]{1,0:T(8,128)S(1)}, f32[208,512]{1,0:T(8,128)S(1)}, u32[]{:S(2)}, u32[]{:S(2)}) %collective-permute-start.1) | collective-permute-done | bytes 426016 | tf_op jit(solution)/shard_map/ppermute | solution.py:15
  73.3 0.3 fusion.13
  73.6 0.1 collective-permute-start.2
  73.7 3.8 %collective-permute-start.3 = (f32[208,128]{1,0:T(8,128)S(1)}, f32[208,128]{1,0:T(8,128)S(1)}, u32[]{:S(2)}, u32[]{:S(2)}) collective-permute-start(f32[208,128]{1,0:T(8,128)S(1)} %get-tuple-element.12), channel_id=1, source_target_pairs={{2,0},{4,2},{6,4},{0,6},{3,1},{5,3},{7,5},{1,7},{10,8},{12,10},{14... | collective-permute-start | bytes 319496 | tf_op jit(solution)/shard_map/ppermute | solution.py:26
  77.5 0.0 copy-done.11
  77.5 0.0 copy-done.1
  77.5 2.7 %collective-permute-done.2 = f32[208,128]{1,0:T(8,128)S(1)} collective-permute-done((f32[208,128]{1,0:T(8,128)S(1)}, f32[208,128]{1,0:T(8,128)S(1)}, u32[]{:S(2)}, u32[]{:S(2)}) %collective-permute-start.2) | collective-permute-done | bytes 106528 | tf_op jit(solution)/shard_map/ppermute | solution.py:25
  80.2 0.0 collective-permute-start.5
  80.2 0.0 collective-permute-done.3
  80.2 0.1 reshape.15
  80.3 0.6 convolution_bitcast_fusion.1
  80.9 0.0 copy-done
  80.9 0.0 slice-start
  80.9 0.0 copy-start.2
  80.9 0.0 copy-start.6
  80.9 0.0 copy-start.7
  80.9 0.6 convolution_bitcast_fusion
  81.5 0.9 copy.77
  82.5 1.9 %reshape_reshape.3 = f32[26,8,512]{2,1,0:T(8,128)} reshape(f32[208,4,128]{2,1,0:T(4,128)} %copy.77) | data formatting | bytes 851968 | tf_op jit(solution)/shard_map/reshape;reshape | solution.py:99
  84.4 1.9 %fusion.12 = f32[26,1,8,512]{3,0,2,1:T(8,128)S(1)} fusion(f32[26,8,512]{2,1,0:T(8,128)} %param.18, f32[26,8,512]{2,0,1:T(8,128)} %copy-done.4, f32[26,8,512]{2,1,0:T(8,128)} %reshape_reshape.3, pred[]{:T(512)S(6)} %eq.12, pred[]{:T(512)S(6)} %eq.11), kind=kLoop, calls=%fused_computation.30 | loop fusion | flops 212992 | bytes 1703938 | tf_op jit(solution)/shard_map/broadcast_in_dim | solution.py:103
  86.3 0.0 collective-permute-done.4
  86.3 3.4 %collective-permute-done.5 = f32[26,4,8,1]{3,0,2,1:T(8,128)} collective-permute-done((f32[26,4,8,1]{3,0,2,1:T(8,128)}, f32[26,4,8,1]{3,0,2,1:T(8,128)}, u32[]{:S(2)}, u32[]{:S(2)}) %collective-permute-start.5) | collective-permute-done | bytes 3360 | tf_op jit(solution)/shard_map/ppermute | solution.py:26
  89.7 0.0 collective-permute-done.6
  89.7 0.0 collective-permute-done.7
  89.7 0.0 slice-done
  89.7 0.0 copy-done.2
  89.7 0.0 copy-done.6
  89.7 0.0 copy-done.7
  89.7 0.0 copy-done.5
  89.7 6.1 %fusion.4 = f32[26,4,8,512]{3,0,2,1:T(8,128)S(1)} fusion(f32[26,4,8,512]{3,0,2,1:T(8,128)} %copy-done.1, f32[26,4,1,512]{3,0,2,1:T(8,128)} %collective-permute-done.7, f32[26,4,1,512]{3,0,2,1:T(8,128)} %collective-permute-done.6, f32[26,4,8,1]{3,0,2,1:T(8,128)} %collective-permute-done.5, f32[26,4,8,1]{3,0,2,1:T(8,128)} %collective-permute-done.4, ...), kind=kLoop, calls=%fused_computation.5 | loop fusion | flops 7667712 | bytes 7444992 | tf_op jit(solution)/shard_map/add | solution.py:122
  95.8 2.2 %copy.94 = f32[26,4,8,512]{3,2,1,0:T(8,128)} copy(f32[26,4,8,512]{3,0,2,1:T(8,128)S(1)} %fusion.4) | data formatting | bytes 3407872 | tf_op jit(solution)/shard_map/add | solution.py:122
  (9 shorter events, 0.1 us)
Async XLA Ops:
  0.0 80.9 %copy-start = (f32[4,128,128]{2,1,0:T(8,128)S(1)}, f32[4,128,128]{2,1,0:T(8,128)}, u32[]{:S(2)}) copy-start(f32[4,128,128]{2,1,0:T(8,128)} %param.19) | copy-start | bytes 786436
  2.5 75.0 %copy-start.1 = (f32[26,4,8,512]{3,0,2,1:T(8,128)}, f32[26,4,8,512]{3,0,2,1:T(8,128)S(1)}, u32[]{:S(2)}) copy-start(f32[26,4,8,512]{3,0,2,1:T(8,128)S(1)} %copy.82) | copy-start | bytes 5111812
  2.6 10.5 %collective-permute-start = (f32[26,8,512]{2,0,1:T(8,128)S(1)}, f32[26,8,512]{2,0,1:T(8,128)S(1)}, u32[]{:S(2)}, u32[]{:S(2)}) collective-permute-start(f32[26,8,512]{2,0,1:T(8,128)S(1)} %slice_bitcast_fusion.2), channel_id=1, source_target_pairs={{0,8},{8,16},{16,24},{1,9},{9,17},{17,25},{2,10},{10,18},{18,26},{... | collective-permute-start | bytes 1277960 | tf_op jit(solution)/shard_map/ppermute | solution.py:34
  13.1 0.8 copy-start.4
  15.1 25.0 %all-to-all-start = ((f32[1,208,512]{1,0,2:T(1,128)}), f32[1,208,512]{1,0,2:T(1,128)S(1)}, u32[]{:S(2)}, u32[]{:S(2)}) async-start(f32[1,208,512]{1,0,2:T(1,128)} %copy.73), calls=%async_computation | async-start | bytes 1048576 | tf_op jit(solution)/shard_map/all_to_all | solution.py:42
  20.8 68.8 %collective-permute-start.6 = (f32[26,4,1,512]{3,0,2,1:T(8,128)}, f32[26,4,1,512]{3,0,2,1:T(8,128)}, u32[]{:S(2)}, u32[]{:S(2)}) collective-permute-start(f32[26,4,1,512]{3,0,2,1:T(8,128)} %get-tuple-element.7), channel_id=1, source_target_pairs={{1,0},{3,2},{5,4},{7,6},{9,8},{11,10},{13,12},{15,14},{17,16},{19,... | collective-permute-start | bytes 638984 | tf_op jit(solution)/shard_map/ppermute | solution.py:26
  22.1 23.5 %copy-start.9 = (f32[6]{0:T(128)S(1)}, f32[6]{0:T(128)}, u32[]{:S(2)}) copy-start(f32[6]{0:T(128)} %param.17) | copy-start | bytes 76
  22.1 23.5 %copy-start.10 = (f32[6]{0:T(128)S(1)}, f32[6]{0:T(128)}, u32[]{:S(2)}) copy-start(f32[6]{0:T(128)} %param.16) | copy-start | bytes 76
  22.2 67.5 %collective-permute-start.7 = (f32[26,4,1,512]{3,0,2,1:T(8,128)}, f32[26,4,1,512]{3,0,2,1:T(8,128)}, u32[]{:S(2)}, u32[]{:S(2)}) collective-permute-start(f32[26,4,1,512]{3,0,2,1:T(8,128)} %get-tuple-element.8), channel_id=1, source_target_pairs={{0,1},{2,3},{4,5},{6,7},{8,9},{10,11},{12,13},{14,15},{16,17},{18,... | collective-permute-start | bytes 638984 | tf_op jit(solution)/shard_map/ppermute | solution.py:25
  29.4 56.9 %collective-permute-start.4 = (f32[26,4,8,1]{3,0,2,1:T(8,128)}, f32[26,4,8,1]{3,0,2,1:T(8,128)}, u32[]{:S(2)}, u32[]{:S(2)}) collective-permute-start(f32[26,4,8,1]{3,0,2,1:T(8,128)} %get-tuple-element.5), channel_id=1, source_target_pairs={{0,2},{2,4},{4,6},{6,0},{1,3},{3,5},{5,7},{7,1},{8,10},{10,12},{12... | collective-permute-start | bytes 9992 | tf_op jit(solution)/shard_map/ppermute | solution.py:25
  41.3 17.2 %all-to-all-start.1 = ((f32[4,208,128]{2,1,0:T(8,128)}), f32[4,208,128]{2,1,0:T(8,128)S(1)}, u32[]{:S(2)}, u32[]{:S(2)}) async-start(f32[4,208,128]{2,1,0:T(8,128)} %fusion.14), calls=%async_computation.1 | async-start | bytes 851968 | tf_op jit(solution)/shard_map/all_to_all | solution.py:45
  58.5 1.3 %copy-start.3 = (f32[20,32,512]{2,1,0:T(8,128)S(1)}, f32[20,32,512]{2,1,0:T(8,128)}, u32[]{:S(2)}) copy-start(f32[20,32,512]{2,1,0:T(8,128)} %slice_bitcast_fusion.1) | copy-start | bytes 3932164
  58.5 1.5 %copy-start.8 = (f32[20,20]{1,0:T(8,128)S(1)}, f32[20,20]{1,0:T(8,128)}, u32[]{:S(2)}) copy-start(f32[20,20]{1,0:T(8,128)} %param.15) | copy-start | bytes 4804
  58.7 14.5 %collective-permute-start.1 = (f32[208,512]{1,0:T(8,128)S(1)}, f32[208,512]{1,0:T(8,128)S(1)}, u32[]{:S(2)}, u32[]{:S(2)}) collective-permute-start(f32[208,512]{1,0:T(8,128)S(1)} %bitcast.60), channel_id=1, source_target_pairs={{6,0},{0,2},{2,4},{4,6},{7,1},{1,3},{3,5},{5,7},{14,8},{8,10},{10,... | collective-permute-start | bytes 1277960 | tf_op jit(solution)/shard_map/ppermute | solution.py:15
  60.0 17.5 %copy-start.11 = (s32[4]{0:T(128)S(1)}, s32[4]{0:T(128)}, u32[]{:S(2)}) copy-start(s32[4]{0:T(128)} %param.20) | copy-start | bytes 52
  73.6 6.6 %collective-permute-start.2 = (f32[208,128]{1,0:T(8,128)S(1)}, f32[208,128]{1,0:T(8,128)S(1)}, u32[]{:S(2)}, u32[]{:S(2)}) collective-permute-start(f32[208,128]{1,0:T(8,128)S(1)} %get-tuple-element.11), channel_id=1, source_target_pairs={{0,2},{2,4},{4,6},{6,0},{1,3},{3,5},{5,7},{7,1},{8,10},{10,12},{12... | collective-permute-start | bytes 319496 | tf_op jit(solution)/shard_map/ppermute | solution.py:25
  73.7 6.5 %collective-permute-start.3 = (f32[208,128]{1,0:T(8,128)S(1)}, f32[208,128]{1,0:T(8,128)S(1)}, u32[]{:S(2)}, u32[]{:S(2)}) collective-permute-start(f32[208,128]{1,0:T(8,128)S(1)} %get-tuple-element.12), channel_id=1, source_target_pairs={{2,0},{4,2},{6,4},{0,6},{3,1},{5,3},{7,5},{1,7},{10,8},{12,10},{14... | collective-permute-start | bytes 319496 | tf_op jit(solution)/shard_map/ppermute | solution.py:26
  80.2 9.5 %collective-permute-start.5 = (f32[26,4,8,1]{3,0,2,1:T(8,128)}, f32[26,4,8,1]{3,0,2,1:T(8,128)}, u32[]{:S(2)}, u32[]{:S(2)}) collective-permute-start(f32[26,4,8,1]{3,0,2,1:T(8,128)} %get-tuple-element.6), channel_id=1, source_target_pairs={{2,0},{4,2},{6,4},{0,6},{3,1},{5,3},{7,5},{1,7},{10,8},{12,10},{14... | collective-permute-start | bytes 9992 | tf_op jit(solution)/shard_map/ppermute | solution.py:26
  80.9 8.8 %slice-start = ((f32[26,4,8,512]{3,0,2,1:T(8,128)}), f32[26,3,8,512]{3,0,2,1:T(8,128)S(1)}, s32[]{:S(2)}) async-start(f32[26,4,8,512]{3,0,2,1:T(8,128)} %copy-done.1), calls=%async_computation.2 | async-start | bytes 3145728 | tf_op jit(solution)/shard_map/slice | solution.py:103
  80.9 8.8 %copy-start.2 = (f32[20,4,8,512]{3,0,2,1:T(8,128)S(1)}, f32[20,4,8,512]{3,0,2,1:T(8,128)}, u32[]{:S(2)}) copy-start(f32[20,4,8,512]{3,0,2,1:T(8,128)} %fusion.9) | copy-start | bytes 3932164
  80.9 8.8 %copy-start.6 = (f32[4,8,512]{2,1,0:T(8,128)S(1)}, f32[4,8,512]{2,1,0:T(8,128)}, u32[]{:S(2)}) copy-start(f32[4,8,512]{2,1,0:T(8,128)} %param.14) | copy-start | bytes 196612
  80.9 8.8 %copy-start.7 = (f32[4,8,512]{2,1,0:T(8,128)S(1)}, f32[4,8,512]{2,1,0:T(8,128)}, u32[]{:S(2)}) copy-start(f32[4,8,512]{2,1,0:T(8,128)} %param.13) | copy-start | bytes 196612
  84.4 5.3 %copy-start.5 = (f32[6,4,8,512]{3,0,2,1:T(8,128)S(1)}, f32[6,4,8,512]{3,0,2,1:T(8,128)}, u32[]{:S(2)}) copy-start(f32[6,4,8,512]{3,0,2,1:T(8,128)} %fusion.11) | copy-start | bytes 1179652
where the time goes:
time: 98.5 us; the launch traced here: 98 us
  waiting for transfers between devices  42.1 us (43%)
  starting transfers between devices  23.6 us (24%)
  local copies, waits for them, and re-layouts  16.9 us (17%)
  other arithmetic  10.1 us (10%)
  matrix products  4.31 us (4%)
  between operations  0.99 us (1%)
    ppermute x1, waiting for transfers between devices, from_behind(): return lax.ppermute(block, axis, route)  10.1 us
    all_to_all x1, waiting for transfers between devices, rotate_rows(): lax.all_to_all(turned, 'theta', split_axis=0, concat_axis=2, tiled=True)[0]  9.34 us
    ppermute x1, waiting for transfers between devices, from_behind_2(): return lax.ppermute(array, axis, pairs)  8.57 us
    ppermute x3, starting transfers between devices, padded(): before = lax.ppermute(last, axis, up)  8.16 us
    all_to_all x1, waiting for transfers between devices, rotate_rows(): lax.all_to_all(plane_rows[None], 'theta', split_axis=2, concat_axis=0, ti...  8.06 us
    unnamed x27, local copies, waits for them, and re-layouts  6.92 us
    add x1, other arithmetic, local(): scalars - axial_speed * (scalars - upstream) + mixing * laplace_term  6.1 us
    ppermute x3, starting transfers between devices, padded(): after = lax.ppermute(initial, axis, down)  5.09 us
  transfers between devices with their start and end apart: 10, of which 6 were waited for; matrix products, arithmetic and copies ran while one was open for 18% of the time, Pallas kernels for 0%

commit v1 on v0

v1 whole, which is shorter than its diff:
```python
import functools

import jax
import jax.numpy as jnp
from jax import lax
from jax.experimental import pallas as pl
from jax.experimental.pallas import tpu as pltpu
from jax.sharding import PartitionSpec as P

SPECIES = 20
TILE = 128
MAX_DIRECT = 8

highest = lax.Precision.HIGHEST


def whole(shape):
    return pl.BlockSpec(shape, lambda *_: (0,) * len(shape))


def smem():
    return pl.BlockSpec(memory_space=pltpu.SMEM)


def pack_kernel(x_ref, plane_ref, low_ref, high_ref, first_ref, last_ref, bottom_ref, top_ref):
    variables, layers, radial_cells, theta_cells = x_ref.shape
    half = theta_cells // 2
    plane = x_ref[:, layers - 1]
    plane_ref[...] = plane
    low_ref[...] = plane[:, :, :half]
    high_ref[...] = plane[:, :, half:]
    lane = lax.broadcasted_iota(jnp.int32, (radial_cells, TILE), 1)
    for block in range(first_ref.shape[1] // TILE):
        first = jnp.zeros((radial_cells, TILE), jnp.float32)
        last = jnp.zeros((radial_cells, TILE), jnp.float32)
        for c in range(block * TILE, min((block + 1) * TILE, layers * variables)):
            a, v = divmod(c, variables)
            where = c % TILE
            head = x_ref[v, a, :, :TILE]
            tail = x_ref[v, a, :, theta_cells - TILE :]
            if where:
                head = pltpu.roll(head, where, 1)
            if (where + 1) % TILE:
                tail = pltpu.roll(tail, (where + 1) % TILE, 1)
            first = jnp.where(lane == where, head, first)
            last = jnp.where(lane == where, tail, last)
        first_ref[:, block * TILE : (block + 1) * TILE] = first
        last_ref[:, block * TILE : (block + 1) * TILE] = last
    for a in range(layers):
        for v in range(variables):
            row = a * variables + v
            bottom_ref[row : row + 1, :] = x_ref[v, a, 0:1, :]
            top_ref[row : row + 1, :] = x_ref[v, a, radial_cells - 1 : radial_cells, :]


def pack(scalars):
    variables, layers, radial_cells, theta_cells = scalars.shape
    half = theta_cells // 2
    lanes = -(-variables * layers // TILE) * TILE
    shapes = [
        (variables, radial_cells, theta_cells),
        (variables, radial_cells, half),
        (variables, radial_cells, half),
        (radial_cells, lanes),
        (radial_cells, lanes),
        (variables * layers, theta_cells),
        (variables * layers, theta_cells),
    ]
    return pl.pallas_call(
        pack_kernel,
        out_shape=[jax.ShapeDtypeStruct(s, jnp.float32) for s in shapes],
        grid=(1,),
        in_specs=[whole(scalars.shape)],
        out_specs=[whole(s) for s in shapes],
        name="pack",
    )(scalars)


def stencil_kernel(
    x_ref, previous_ref, speed_ref, mixing_ref, rate_ref,
    before_ref, after_ref, below_ref, above_ref,
    reaction_ref, nucleation_ref, coagulation_ref, out_ref,
):
    variables, _, radial_cells, theta_cells = x_ref.shape
    layer = pl.program_id(0)
    position = lax.axis_index("radial")
    blocks = lax.axis_size("radial")
    speed, mixing, rate = speed_ref[0], mixing_ref[0], rate_ref[0]
    lane = lax.broadcasted_iota(jnp.int32, (radial_cells, theta_cells), 1)
    row = lax.broadcasted_iota(jnp.int32, (radial_cells, theta_cells), 0)
    inner = jnp.broadcast_to(layer > 0, (radial_cells, theta_cells))
    open_below = jnp.broadcast_to(position > 0, (1, theta_cells))
    open_above = jnp.broadcast_to(position < blocks - 1, (1, theta_cells))
    offset = layer * variables

    def column(ref, v, target):
        c = offset + v
        tile = ref[:, :TILE]
        if ref.shape[1] > TILE:
            tile = ref[:, pl.ds(pl.multiple_of(c // TILE * TILE, TILE), TILE)]
        return pltpu.roll(tile, (target - c % TILE + TILE) % TILE, 1)

    def advance(v, source):
        x = x_ref[v, 0]
        previous = column(before_ref, v, 0)
        following = column(after_ref, v, TILE - 1)
        spread = [previous] + [previous] * (theta_cells // TILE - 1)
        left = jnp.where(lane == 0, jnp.concatenate(spread, axis=1), pltpu.roll(x, 1, 1))
        spread = [following] * (theta_cells // TILE)
        right = jnp.where(
            lane == theta_cells - 1, jnp.concatenate(spread, axis=1), pltpu.roll(x, theta_cells - 1, 1)
        )
        wall = jnp.zeros((1, theta_cells), jnp.float32)
        below = jnp.where(open_below, below_ref[pl.ds(offset + v, 1), :], wall)
        above = jnp.where(open_above, above_ref[pl.ds(offset + v, 1), :], wall)
        down = jnp.where(row == 0, below, pltpu.roll(x, 1, 0))
        up = jnp.where(row == radial_cells - 1, above, pltpu.roll(x, radial_cells - 1, 0))
        laplace = left + right + up + down - 4.0 * x
        upstream = jnp.where(inner, previous_ref[v, 0], 0.0)
        out_ref[v, 0] = x - speed * (x - upstream) + mixing * laplace + source * rate

    chunk = 5
    for start in range(0, SPECIES, chunk):
        totals = [jnp.zeros((radial_cells, theta_cells), jnp.float32)] * chunk
        for j in range(SPECIES):
            x = x_ref[j, 0]
            totals = [t + reaction_ref[start + i, j] * x for i, t in enumerate(totals)]
        for i, total in enumerate(totals):
            advance(start + i, total)
    final = x_ref[SPECIES - 1, 0]
    zeroth = x_ref[SPECIES, 0]
    for k in range(variables - SPECIES):
        moment = x_ref[SPECIES + k, 0]
        advance(SPECIES + k, nucleation_ref[k] * final - coagulation_ref[k] * zeroth * moment)


def stencil(scalars, speed, mixing, rate, before, after, below, above, reaction, nucleation, coagulation):
    variables, layers, radial_cells, theta_cells = scalars.shape
    block = (variables, 1, radial_cells, theta_cells)
    cell = pl.BlockSpec((1, radial_cells, theta_cells), lambda a: (a, 0, 0))
    return pl.pallas_call(
        stencil_kernel,
        out_shape=jax.ShapeDtypeStruct(scalars.shape, jnp.float32),
        grid=(layers,),
        in_specs=[
            pl.BlockSpec(block, lambda a: (0, a, 0, 0)),
            pl.BlockSpec(block, lambda a: (0, jnp.maximum(a - 1, 0), 0, 0)),
            cell, cell, cell,
            whole(before.shape), whole(after.shape), whole(below.shape), whole(above.shape),
            smem(), smem(), smem(),
        ],
        out_specs=pl.BlockSpec(block, lambda a: (0, a, 0, 0)),
        cost_estimate=pl.CostEstimate(flops=40_000_000, bytes_accessed=5_000_000, transcendentals=0),
        name="stencil",
    )(scalars, scalars, speed, mixing, rate, before, after, below, above, reaction, nucleation, coagulation)


def finish_kernel(count, start_of, partial_ref, speed_ref, inflow_ref, direct_ref, *refs):
    piece_refs = refs[:count]
    weights_ref, donor_ref, rotor_ref, out_ref, side_ref, window_ref = refs[count:]
    variables, _, radial_cells, theta_cells = partial_ref.shape
    group, groups = lax.axis_index("group"), lax.axis_size("group")
    tiles = theta_cells // TILE
    speed = speed_ref[0]
    rows = variables * radial_cells

    @pl.when(group == 0)
    def _():
        for v in range(variables):
            out_ref[v, 0] = partial_ref[v, 0] + speed * inflow_ref[v]

    @pl.when(jnp.logical_and(group > 0, group < groups - 1))
    def _():
        for v in range(variables):
            out_ref[v, 0] = partial_ref[v, 0] + speed * direct_ref[v]

    @pl.when(group == groups - 1)
    def _():
        at = 0
        for ref in piece_refs:
            width = ref.shape[2]
            side_ref[:, :, at : at + width] = ref[...]
            at += width
        start = start_of(rotor_ref[0])
        first, turn = start // TILE, start % TILE
        lane = lax.broadcasted_iota(jnp.int32, (rows, TILE), 1)
        back = (TILE - turn) % TILE

        def tile(m):
            position = jnp.minimum(first + m, at // TILE - 1) * TILE
            block = side_ref[:, :, pl.ds(pl.multiple_of(position, TILE), TILE)]
            return pltpu.roll(block.reshape(rows, TILE), back, 1)

        here = tile(0)
        for m in range(tiles + 2):
            there = tile(m + 1)
            window_ref[m] = jnp.where(lane < TILE - turn, here, there)
            here = there
        for t in range(tiles):
            donor = window_ref[t + 1 + donor_ref[t]]
            ghost = lax.dot_general(
                donor, weights_ref[t], (((1,), (1,)), ((), ())),
                precision=highest, preferred_element_type=jnp.float32,
            ).reshape(variables, radial_cells, TILE)
            span = slice(t * TILE, (t + 1) * TILE)
            out_ref[:, 0, :, span] = partial_ref[:, 0, :, span] + speed[:, span] * ghost


def finish(partial, speed, inflow, direct, pieces, start_of, weights, donor_shift, rotor_offset):
    variables, layers, radial_cells, theta_cells = partial.shape
    steps = 2 if variables % 2 == 0 else 1
    part = variables // steps
    width = sum(p.shape[2] for p in pieces)
    tiles = theta_cells // TILE
    first_layer = pl.BlockSpec((part, 1, radial_cells, theta_cells), lambda i: (i, 0, 0, 0))
    plane = lambda cells: pl.BlockSpec((part, radial_cells, cells), lambda i: (i, 0, 0))
    return pl.pallas_call(
        functools.partial(finish_kernel, len(pieces), start_of),
        out_shape=jax.ShapeDtypeStruct(partial.shape, jnp.float32),
        grid=(steps,),
        in_specs=[
            first_layer,
            pl.BlockSpec((1, radial_cells, theta_cells), lambda i: (0, 0, 0)),
            plane(theta_cells), plane(theta_cells),
            *[plane(p.shape[2]) for p in pieces],
            whole(weights.shape), smem(), smem(),
        ],
        out_specs=first_layer,
        scratch_shapes=[
            pltpu.VMEM((part, radial_cells, width), jnp.float32),
            pltpu.VMEM((tiles + 2, part * radial_cells, TILE), jnp.float32),
        ],
        input_output_aliases={0: 0},
        cost_estimate=pl.CostEstimate(flops=100_000_000, bytes_accessed=3_000_000, transcendentals=0),
        name="finish",
    )(partial, speed, inflow, direct, *pieces, weights, donor_shift, rotor_offset)


def ring(block, axis, by):
    count = lax.axis_size(axis)
    return lax.ppermute(block, axis, [(i, (i + by) % count) for i in range(count)])


def radial_halos(bottom, top):
    count = lax.axis_size("radial")
    if count == 2:
        sent = jnp.where(lax.axis_index("radial") == 0, top, bottom)
        got = lax.ppermute(sent, "radial", [(0, 1), (1, 0)])
        return got, got
    up = [(i, i + 1) for i in range(count - 1)]
    below = lax.ppermute(top, "radial", up)
    above = lax.ppermute(bottom, "radial", [(j, i) for i, j in up])
    return below, above


def downstream(block, by, others=False):
    groups, sectors = lax.axis_size("group"), lax.axis_size("theta")
    pairs = []
    for g in range(groups - 1):
        for s in range(sectors):
            if g == groups - 2:
                pairs.append((g * sectors + s, (g + 1) * sectors + (s + by) % sectors))
            elif others:
                pairs.append((g * sectors + s, (g + 1) * sectors + s))
    return lax.ppermute(block, ("group", "theta"), pairs)


def rotated_plane(plane, rotor_offset):
    variables, radial_cells, theta_cells = plane.shape
    sectors = lax.axis_size("theta")
    rows = plane.reshape(variables * radial_cells, theta_cells)
    hops, shift = rotor_offset[0] // theta_cells, rotor_offset[0] % theta_cells
    scattered = lax.all_to_all(rows[None], "theta", split_axis=2, concat_axis=0, tiled=True)
    doubled = jnp.concatenate([scattered, scattered], axis=0)
    turned = lax.dynamic_slice_in_dim(doubled, sectors - hops, sectors, 0)
    shifted = lax.all_to_all(turned, "theta", split_axis=0, concat_axis=2, tiled=True)[0]
    joined = jnp.concatenate([ring(shifted, "theta", 1), shifted], axis=1)
    rotated = lax.dynamic_slice_in_dim(joined, theta_cells - shift, theta_cells, 1)
    return rotated.reshape(plane.shape)


def local(
    scalars, axial_speed, mixing, reaction_rate, reaction, nucleation, coagulation,
    inflow, tile_weights, donor_shift, rotor_offset,
):
    theta_cells = scalars.shape[3]
    sectors = lax.axis_size("theta")
    half = theta_cells // 2
    plane, low, high, first, last, bottom, top = pack(scalars)

    def inner():
        before, after = ring(last, "theta", 1), ring(first, "theta", -1)
        below, above = radial_halos(bottom, top)
        return stencil(
            scalars, axial_speed, mixing, reaction_rate, before, after, below, above,
            reaction, nucleation, coagulation,
        )

    def closing(partial, direct, pieces, start_of):
        return finish(
            partial, axial_speed, inflow, direct, pieces, start_of, tile_weights, donor_shift, rotor_offset
        )

    if sectors > MAX_DIRECT or half % TILE or theta_cells < 4 * TILE:
        direct = downstream(plane, 0, others=True)
        rotated = rotated_plane(direct, rotor_offset)
        pieces = [
            ring(rotated[:, :, theta_cells - TILE :], "theta", 1),
            rotated,
            ring(rotated[:, :, :TILE], "theta", -1),
        ]
        return closing(inner(), direct, pieces, lambda offset: jnp.int32(0))

    def branch(hops, late):
        def run():
            block = downstream(plane, hops, others=True)
            if late:
                pieces = [downstream(plane, hops + 1), block]
                length = theta_cells
            else:
                pieces = [downstream(high, hops + 1), block, downstream(low, hops - 1)]
                length = half
            return closing(
                inner(), block, pieces, lambda offset: length - (offset + TILE) % theta_cells
            )

        return run

    reach = rotor_offset[0] + TILE
    hops = (reach // theta_cells) % sectors
    late = reach % theta_cells > half
    index = hops * 2 + late.astype(jnp.int32)
    return lax.switch(index, [branch(h, c) for h in range(sectors) for c in (False, True)])


def solution(mesh):
    placed = (
        P(None, "group", "radial", "theta"),
        P("group", "radial", "theta"),
        P("group", "radial", "theta"),
        P("group", "radial", "theta"),
        P(),
        P(),
        P(),
        P(None, "radial", "theta"),
        P("theta", None, None),
        P("theta"),
        P(),
    )
    return jax.shard_map(
        local,
        mesh=mesh,
        in_specs=placed,
        out_specs=P(None, "group", "radial", "theta"),
        check_vma=False,
    )
```

time: 98.5 us -> 34.2 us (0.35)
  the two profiles are of different devices: /device:TPU:2 before, /device:TPU:18 now
where the time goes in v1:
time: 34.2 us; the launch traced here: 34.1 us
  waiting for transfers between devices  12.1 us (35%)
  Pallas kernels  11.4 us (33%)
  starting transfers between devices  7.73 us (23%)
  local copies, waits for them, and re-layouts  1.61 us (5%)
  between operations  0.88 us (3%)
    ppermute x2, waiting for transfers between devices, ring(): lax.ppermute(block, axis, [(i, (i + by) % count) for i in range(count)])  12.1 us
    pallas_call x1, Pallas kernels, stencil(): pl.pallas_call(stencil_kernel, out_shape=jax.ShapeDtypeStruct(scalars.sha...  5.77 us
    ppermute x3, starting transfers between devices, downstream(): return lax.ppermute(block, ('group', 'theta'), pairs)  4.51 us
    pallas_call x1, Pallas kernels, finish(): pl.pallas_call(functools.partial(finish_kernel, len(pieces), start_of), o...  2.91 us
    pallas_call x1, Pallas kernels, pack(): pl.pallas_call(pack_kernel, out_shape=[jax.ShapeDtypeStruct(s, jnp.float3...  2.71 us
    ppermute x2, starting transfers between devices, ring(): lax.ppermute(block, axis, [(i, (i + by) % count) for i in range(count)])  1.63 us
    cond x16, local copies, waits for them, and re-layouts  1.59 us
    ppermute x1, starting transfers between devices, radial_halos(): got = lax.ppermute(sent, 'radial', [(0, 1), (1, 0)])  1.58 us
  transfers between devices with their start and end apart: 6, of which 2 were waited for; matrix products, arithmetic and copies ran while one was open for 0% of the time, Pallas kernels for 17%

profile of v1, /device:TPU:18, one launch (start us, length us, event | category | flops | bytes accessed | tf_op | source)
XLA Modules:
  0.0 34.1 jit_solution(4263143963944079051)
XLA Ops:
  0.0 0.0 copy-start
  0.0 0.0 copy-start.43
  0.0 0.0 copy-start.45
  0.0 0.0 copy-start.44
  0.0 0.0 copy-start.34
  0.0 0.0 copy-start.9
  0.9 2.7 %pack.1 = (f32[26,8,512]{2,1,0:T(8,128)}, f32[26,8,256]{2,1,0:T(8,128)}, f32[26,8,256]{2,1,0:T(8,128)}, f32[8,128]{1,0:T(8,128)S(1)}, f32[8,128]{1,0:T(8,128)S(1...) custom-call(f32[26,4,8,512]{3,2,1,0:T(8,128)} %x_ref.1), custom_call_target="tpu_custom_call" | custom-call | tf_op jit(solution)/shard_map/pack/pallas_call | solution.py:69
  3.6 0.0 copy-done
  3.6 0.0 copy-done.43
  3.6 0.0 copy-done.45
  3.6 0.0 copy-done.44
  3.6 0.0 copy-done.34
  3.6 0.0 copy-done.9
  3.6 30.5 %conditional.1 = (f32[26,4,8,512]{3,2,1,0:T(8,128)}) conditional(s32[]{:T(128)} %clamp.3, (f32[8,128]{1,0:T(8,128)S(1)}, f32[8,128]{1,0:T(8,128)S(1)}, f32[104,512]{1,0:T(8,128)S(1)}, f32[104,512]{1,0:T(8,128)S(1)}, f32[26,4,8,512]{3,2,1,0:T(8,128)S(1)}, /*index=5*/f32[4,8,512]{2,1,0:T(8,128)S(1)}, ...), branch_computations={%region_0.1_spmd, %region_1.2_spmd, %region_2.3_spmd, %region_3.4_... | conditional | flops 140053248 | bytes 19977206 | solution.py:333
  3.8 1.9 %collective-permute-start.36 = (f32[26,8,512]{2,1,0:T(8,128)}, f32[26,8,512]{2,1,0:T(8,128)S(1)}, u32[]{:S(2)}, u32[]{:S(2)}) collective-permute-start(f32[26,8,512]{2,1,0:T(8,128)} %get-tuple-element.400), channel_id=1, source_target_pairs={{0,8},{2,10},{4,12},{6,14},{8,16},{10,18},{12,20},{14,22},{16,30},... | collective-permute-start | bytes 1277960 | tf_op jit(solution)/shard_map/cond/branch_6_fun/ppermute | solution.py:265
  5.8 1.6 %collective-permute-start.35 = (f32[104,512]{1,0:T(8,128)S(1)}, f32[104,512]{1,0:T(8,128)S(1)}, u32[]{:S(2)}, u32[]{:S(2)}) collective-permute-start(f32[104,512]{1,0:T(8,128)S(1)} %broadcast_select_fusion.6), channel_id=1, source_target_pairs={{0,1},{1,0},{2,3},{3,2},{4,5},{5,4},{6,7},{7,6},{8,9},{9,8},{10,11... | collective-permute-start | bytes 638984 | tf_op jit(solution)/shard_map/cond/branch_6_fun/ppermute | solution.py:248
  7.4 1.3 %collective-permute-start.37 = (f32[26,8,256]{2,1,0:T(8,128)}, f32[26,8,256]{2,1,0:T(8,128)S(1)}, u32[]{:S(2)}, u32[]{:S(2)}) collective-permute-start(f32[26,8,256]{2,1,0:T(8,128)} %get-tuple-element.401), channel_id=1, source_target_pairs={{16,24},{18,26},{20,28},{22,30},{17,25},{19,27},{21,29},{23,31}} | collective-permute-start | bytes 638984 | tf_op jit(solution)/shard_map/cond/branch_6_fun/ppermute | solution.py:265
  8.7 1.3 %collective-permute-start.38 = (f32[26,8,256]{2,1,0:T(8,128)}, f32[26,8,256]{2,1,0:T(8,128)S(1)}, u32[]{:S(2)}, u32[]{:S(2)}) collective-permute-start(f32[26,8,256]{2,1,0:T(8,128)} %get-tuple-element.402), channel_id=1, source_target_pairs={{16,28},{18,30},{20,24},{22,26},{17,29},{19,31},{21,25},{23,27}} | collective-permute-start | bytes 638984 | tf_op jit(solution)/shard_map/cond/branch_6_fun/ppermute | solution.py:265
  10.0 1.6 %collective-permute-start.33 = (f32[8,128]{1,0:T(8,128)S(1)}, f32[8,128]{1,0:T(8,128)S(1)}, u32[]{:S(2)}, u32[]{:S(2)}) collective-permute-start(f32[8,128]{1,0:T(8,128)S(1)} %get-tuple-element.392), channel_id=1, source_target_pairs={{0,2},{2,4},{4,6},{6,0},{1,3},{3,5},{5,7},{7,1},{8,10},{10,12},{12... | collective-permute-start | bytes 12296 | tf_op jit(solution)/shard_map/cond/branch_6_fun/ppermute | solution.py:241
  11.6 8.5 %collective-permute-done.33.before_ref = f32[8,128]{1,0:T(8,128)S(1)} collective-permute-done((f32[8,128]{1,0:T(8,128)S(1)}, f32[8,128]{1,0:T(8,128)S(1)}, u32[]{:S(2)}, u32[]{:S(2)}) %collective-permute-start.33) | collective-permute-done | bytes 4128 | tf_op jit(solution)/shard_map/cond/branch_6_fun/ppermute | solution.py:241
  20.2 0.0 copy-start.52
  20.2 0.0 collective-permute-start.34
  20.2 3.6 %collective-permute-done.34.after_ref = f32[8,128]{1,0:T(8,128)S(1)} collective-permute-done((f32[8,128]{1,0:T(8,128)S(1)}, f32[8,128]{1,0:T(8,128)S(1)}, u32[]{:S(2)}, u32[]{:S(2)}) %collective-permute-start.34) | collective-permute-done | bytes 4128 | tf_op jit(solution)/shard_map/cond/branch_6_fun/ppermute | solution.py:241
  23.8 0.0 copy-start.61
  23.8 0.0 collective-permute-done.35.below_ref.above_ref
  23.8 0.0 copy-start.29
  23.8 0.0 copy-done.52
  23.8 0.6 %copy-done.61 = f32[8,128]{1,0:T(8,128)} copy-done((f32[8,128]{1,0:T(8,128)}, f32[8,128]{1,0:T(8,128)S(1)}, u32[]{:S(2)}) %copy-start.61) | copy-done | bytes 4120 | tf_op jit(solution)/shard_map/cond
  24.3 0.1 copy-done.29
  24.4 0.0 copy-start.7
  24.4 0.0 copy-start.16
  24.5 5.8 %stencil.14.partial_ref = f32[26,4,8,512]{3,2,1,0:T(8,128)} custom-call(f32[26,4,8,512]{3,2,1,0:T(8,128)S(1)} %get-tuple-element.388.x_ref.previous_ref, f32[26,4,8,512]{3,2,1,0:T(8,128)S(1)} %get-tuple-element.388.x_ref.previous_ref, f32[4,8,512]{2,1,0:T(8,128)S(1)} %get-tuple-element.389.speed_ref, f32[4,8,512]{2,1,0:T(8,128)} %get-tuple-element.390.mixing_ref, ...), custom_call_target="tpu_custom_call" | custom-call | flops 40000000 | bytes 5000000 | tf_op jit(solution)/shard_map/cond/branch_6_fun/stencil/pallas_call | solution.py:141
  30.2 0.0 collective-permute-done.37.refs_0_
  30.2 0.0 copy-start.38
  30.2 0.0 collective-permute-done.38.refs_2_
  30.3 0.0 copy-start.42
  30.3 0.0 collective-permute-done.36.direct_ref.refs_1_
  30.3 0.0 copy-start.21
  30.3 0.6 %copy-done.38 = f32[26,8,256]{2,1,0:T(8,128)} copy-done((f32[26,8,256]{2,1,0:T(8,128)}, f32[26,8,256]{2,1,0:T(8,128)S(1)}, u32[]{:S(2)}) %copy-start.38) | copy-done | bytes 213016 | tf_op jit(solution)/shard_map/cond
  30.9 0.1 copy-done.42
  31.0 0.2 copy-done.21
  31.2 0.0 copy-done.7
  31.2 0.0 copy-done.16
  31.2 2.9 %finish.14 = f32[26,4,8,512]{3,2,1,0:T(8,128)} custom-call(f32[26,4,8,512]{3,2,1,0:T(8,128)} %stencil.14.partial_ref, f32[4,8,512]{2,1,0:T(8,128)S(1)} %get-tuple-element.389.speed_ref, f32[26,8,512]{2,1,0:T(8,128)S(1)} %copy-done.7, f32[26,8,512]{2,1,0:T(8,128)} %copy-done.21, f32[26,8,256]{2,1,0:T(8,128)} %copy-done.38, ...), custom_call_target="tpu_custom_call", output_to_operand_aliasing={{}: (0, {})} | custom-call | flops 100000000 | bytes 3000000 | tf_op jit(solution)/shard_map/cond/branch_6_fun/finish/pallas_call | solution.py:217
  (1 shorter events, 0.0 us)
Async XLA Ops:
  0.0 3.6 %copy-start = (f32[26,4,8,512]{3,2,1,0:T(8,128)S(1)}, f32[26,4,8,512]{3,2,1,0:T(8,128)}, u32[]{:S(2)}) copy-start(f32[26,4,8,512]{3,2,1,0:T(8,128)} %x_ref.1) | copy-start | bytes 5111812
  0.0 3.6 %copy-start.43 = (s32[4]{0:T(128)S(1)}, s32[4]{0:T(128)}, u32[]{:S(2)}) copy-start(s32[4]{0:T(128)} %param.28) | copy-start | bytes 52
  0.0 3.6 %copy-start.45 = (f32[6]{0:T(128)S(1)}, f32[6]{0:T(128)}, u32[]{:S(2)}) copy-start(f32[6]{0:T(128)} %param.25) | copy-start | bytes 76
  0.0 3.6 %copy-start.44 = (f32[6]{0:T(128)S(1)}, f32[6]{0:T(128)}, u32[]{:S(2)}) copy-start(f32[6]{0:T(128)} %param.24) | copy-start | bytes 76
  0.0 3.6 %copy-start.34 = (f32[20,20]{1,0:T(8,128)S(1)}, f32[20,20]{1,0:T(8,128)}, u32[]{:S(2)}) copy-start(f32[20,20]{1,0:T(8,128)} %param.23) | copy-start | bytes 4804
  0.0 3.6 %copy-start.9 = (f32[4,8,512]{2,1,0:T(8,128)S(1)}, f32[4,8,512]{2,1,0:T(8,128)}, u32[]{:S(2)}) copy-start(f32[4,8,512]{2,1,0:T(8,128)} %param.20) | copy-start | bytes 196612
  3.8 26.4 %collective-permute-start.36 = (f32[26,8,512]{2,1,0:T(8,128)}, f32[26,8,512]{2,1,0:T(8,128)S(1)}, u32[]{:S(2)}, u32[]{:S(2)}) collective-permute-start(f32[26,8,512]{2,1,0:T(8,128)} %get-tuple-element.400), channel_id=1, source_target_pairs={{0,8},{2,10},{4,12},{6,14},{8,16},{10,18},{12,20},{14,22},{16,30},... | collective-permute-start | bytes 1277960 | tf_op jit(solution)/shard_map/cond/branch_6_fun/ppermute | solution.py:265
  5.8 18.0 %collective-permute-start.35 = (f32[104,512]{1,0:T(8,128)S(1)}, f32[104,512]{1,0:T(8,128)S(1)}, u32[]{:S(2)}, u32[]{:S(2)}) collective-permute-start(f32[104,512]{1,0:T(8,128)S(1)} %broadcast_select_fusion.6), channel_id=1, source_target_pairs={{0,1},{1,0},{2,3},{3,2},{4,5},{5,4},{6,7},{7,6},{8,9},{9,8},{10,11... | collective-permute-start | bytes 638984 | tf_op jit(solution)/shard_map/cond/branch_6_fun/ppermute | solution.py:248
  7.4 22.8 %collective-permute-start.37 = (f32[26,8,256]{2,1,0:T(8,128)}, f32[26,8,256]{2,1,0:T(8,128)S(1)}, u32[]{:S(2)}, u32[]{:S(2)}) collective-permute-start(f32[26,8,256]{2,1,0:T(8,128)} %get-tuple-element.401), channel_id=1, source_target_pairs={{16,24},{18,26},{20,28},{22,30},{17,25},{19,27},{21,29},{23,31}} | collective-permute-start | bytes 638984 | tf_op jit(solution)/shard_map/cond/branch_6_fun/ppermute | solution.py:265
  8.7 21.6 %collective-permute-start.38 = (f32[26,8,256]{2,1,0:T(8,128)}, f32[26,8,256]{2,1,0:T(8,128)S(1)}, u32[]{:S(2)}, u32[]{:S(2)}) collective-permute-start(f32[26,8,256]{2,1,0:T(8,128)} %get-tuple-element.402), channel_id=1, source_target_pairs={{16,28},{18,30},{20,24},{22,26},{17,29},{19,31},{21,25},{23,27}} | collective-permute-start | bytes 638984 | tf_op jit(solution)/shard_map/cond/branch_6_fun/ppermute | solution.py:265
  10.0 10.2 %collective-permute-start.33 = (f32[8,128]{1,0:T(8,128)S(1)}, f32[8,128]{1,0:T(8,128)S(1)}, u32[]{:S(2)}, u32[]{:S(2)}) collective-permute-start(f32[8,128]{1,0:T(8,128)S(1)} %get-tuple-element.392), channel_id=1, source_target_pairs={{0,2},{2,4},{4,6},{6,0},{1,3},{3,5},{5,7},{7,1},{8,10},{10,12},{12... | collective-permute-start | bytes 12296 | tf_op jit(solution)/shard_map/cond/branch_6_fun/ppermute | solution.py:241
  20.2 3.6 %copy-start.52 = (f32[8,128]{1,0:T(8,128)}, f32[8,128]{1,0:T(8,128)S(1)}, u32[]{:S(2)}) copy-start(f32[8,128]{1,0:T(8,128)S(1)} %collective-permute-done.33.before_ref) | copy-start | bytes 12292 | tf_op jit(solution)/shard_map/cond
  20.2 3.6 %collective-permute-start.34 = (f32[8,128]{1,0:T(8,128)S(1)}, f32[8,128]{1,0:T(8,128)S(1)}, u32[]{:S(2)}, u32[]{:S(2)}) collective-permute-start(f32[8,128]{1,0:T(8,128)S(1)} %get-tuple-element.393), channel_id=1, source_target_pairs={{0,6},{2,0},{4,2},{6,4},{1,7},{3,1},{5,3},{7,5},{8,14},{10,8},{12,... | collective-permute-start | bytes 12296 | tf_op jit(solution)/shard_map/cond/branch_6_fun/ppermute | solution.py:241
  23.8 0.6 %copy-start.61 = (f32[8,128]{1,0:T(8,128)}, f32[8,128]{1,0:T(8,128)S(1)}, u32[]{:S(2)}) copy-start(f32[8,128]{1,0:T(8,128)S(1)} %collective-permute-done.34.after_ref) | copy-start | bytes 12292 | tf_op jit(solution)/shard_map/cond
  23.8 0.7 %copy-start.29 = (f32[104,512]{1,0:T(8,128)}, f32[104,512]{1,0:T(8,128)S(1)}, u32[]{:S(2)}) copy-start(f32[104,512]{1,0:T(8,128)S(1)} %collective-permute-done.35.below_ref.above_ref) | copy-start | bytes 638980 | tf_op jit(solution)/shard_map/cond
  24.4 6.7 %copy-start.7 = (f32[26,8,512]{2,1,0:T(8,128)S(1)}, f32[26,8,512]{2,1,0:T(8,128)}, u32[]{:S(2)}) copy-start(f32[26,8,512]{2,1,0:T(8,128)} %get-tuple-element.399.inflow_ref) | copy-start | bytes 1277956 | tf_op jit(solution)/shard_map/cond
  24.4 6.7 %copy-start.16 = (f32[4,128,128]{2,1,0:T(8,128)S(1)}, f32[4,128,128]{2,1,0:T(8,128)}, u32[]{:S(2)}) copy-start(f32[4,128,128]{2,1,0:T(8,128)} %get-tuple-element.403.refs_3_) | copy-start | bytes 786436 | tf_op jit(solution)/shard_map/cond
  30.2 0.7 %copy-start.38 = (f32[26,8,256]{2,1,0:T(8,128)}, f32[26,8,256]{2,1,0:T(8,128)S(1)}, u32[]{:S(2)}) copy-start(f32[26,8,256]{2,1,0:T(8,128)S(1)} %collective-permute-done.37.refs_0_) | copy-start | bytes 638980 | tf_op jit(solution)/shard_map/cond
  30.3 0.8 %copy-start.42 = (f32[26,8,256]{2,1,0:T(8,128)}, f32[26,8,256]{2,1,0:T(8,128)S(1)}, u32[]{:S(2)}) copy-start(f32[26,8,256]{2,1,0:T(8,128)S(1)} %collective-permute-done.38.refs_2_) | copy-start | bytes 638980 | tf_op jit(solution)/shard_map/cond
  30.3 0.9 %copy-start.21 = (f32[26,8,512]{2,1,0:T(8,128)}, f32[26,8,512]{2,1,0:T(8,128)S(1)}, u32[]{:S(2)}) copy-start(f32[26,8,512]{2,1,0:T(8,128)S(1)} %collective-permute-done.36.direct_ref.refs_1_) | copy-start | bytes 1277956 | tf_op jit(solution)/shard_map/cond
